TPU v7x, 32 devices: a whole 2x2x4 slice. The times are simulated.
32 devices in a mesh: expert: 8 (over z, core), shard: 4 (over y, x).
Axes of the slice: x: 2, y: 2, z: 4, core: 2. Of those that a mesh axis runs over, the one named last changes fastest.
Arguments:
- w_down: float32 [64, 1024, 2048], P('expert', None, 'shard'), may hold values from -0.25 to 0.25
- avg_down: float32 [64, 1024, 2048], P('expert', None, 'shard'), may hold values from -0.1875 to 0.1875
- mix_share: float32 [64], P('expert'), may hold values from 0.2 to 0.8
- router_weight: float32 [2048, 64], P('shard', 'expert'), may hold values from -0.125 to 0.125
- router_gain: float32 [2048], P('shard'), may hold values from 0.25 to 1.75
Outputs:
- serve_down: bfloat16 [64, 1024, 2048], P('expert')
- scale_down: float32 [64, 1024], P('expert')
- serve_router: bfloat16 [2048, 64], replicated
All inputs are finite; a program needn't handle non-finite values. Where the computation divides by a largest or mean magnitude, that divisor is 1e-20 or more.
Results may differ from a plain program's by a relative error of at most 0.001.
Values may be sent and summed in bfloat16 or wider, within the bound.
A program may use at most 192 MiB of HBM per device.

v0:
```python
import jax
import jax.numpy as jnp
from jax import lax
from jax.sharding import PartitionSpec as P

D_MODEL = 2048


def body(w_down, avg_down, mix_share, router_weight, router_gain):
    fresh_down = mix_share[:, None, None] * w_down + (1.0 - mix_share[:, None, None]) * avg_down
    total_down = lax.psum(jnp.sum(jnp.abs(fresh_down), axis=2), "shard")
    scale_down = total_down / D_MODEL
    narrow_down = (fresh_down / jnp.expand_dims(scale_down, 2)).astype(jnp.bfloat16)
    serve_down = lax.all_gather(narrow_down, "shard", axis=2, tiled=True)
    part_router = (router_weight * router_gain[:, None]).astype(jnp.bfloat16)
    row_router = lax.all_gather(part_router, "shard", axis=0, tiled=True)
    serve_router = lax.all_gather(row_router, "expert", axis=1, tiled=True)
    return (serve_down, scale_down, serve_router)


def solution(mesh):
    return jax.shard_map(
        body,
        mesh=mesh,
        in_specs=(
            P("expert", None, "shard"),
            P("expert", None, "shard"),
            P("expert"),
            P("shard", "expert"),
            P("shard"),
        ),
        out_specs=(P("expert", None, None), P("expert", None), P()),
        check_vma=False,
    )
```

profile of v0, /device:TPU:0, one launch (start us, length us, event | category | flops | bytes accessed | tf_op | source)
XLA Modules:
  0.0 381.0 jit_solution(12262605940895177854)
XLA Ops:
  7.2 0.0 all-gather.2.cloned.1.call-start
  7.2 0.7 broadcast_subtract_fusion
  7.9 0.0 copy-start.3
  7.9 13.2 %abs_reduce_fusion = f32[8,1024]{1,0:T(8,128)S(1)} fusion(f32[8,1024,512]{2,1,0:T(8,128)} %param.6, f32[8]{0:T(128)S(1)} %broadcast_subtract_fusion, f32[8,1024,512]{2,1,0:T(8,128)} %param.5, f32[8]{0:T(128)} %param.7), kind=kLoop, calls=%fused_computation.1 | loop fusion | flops 20963328 | bytes 33587264 | tf_op jit(solution)/shard_map/reduce_sum | solution.py:11
  21.1 17.8 %psum.7 = f32[8,1024]{1,0:T(8,128)S(1)} all-reduce(f32[8,1024]{1,0:T(8,128)S(1)} %abs_reduce_fusion), channel_id=1, replica_groups=mesh['expert'=8,'shard'=4] {'shard'}, use_global_device_ids=true, to_apply=%region_1.0 | all-reduce | flops 8192 | bytes 65536 | tf_op jit(solution)/shard_map/psum | solution.py:11
  38.9 0.0 copy-done.3
  38.9 0.0 copy-start
  38.9 0.0 copy-start.1
  38.9 0.0 copy-start.2
  38.9 15.1 %divide_convert_fusion = bf16[8,1024,512]{2,1,0:T(8,128)(2,1)} fusion(f32[8,1024]{1,0:T(8,128)S(1)} %broadcast_multiply_fusion, f32[8,1024,512]{2,1,0:T(8,128)} %param.6, f32[8]{0:T(128)S(1)} %broadcast_subtract_fusion, f32[8,1024,512]{2,1,0:T(8,128)} %param.5, f32[8]{0:T(128)S(1)} %copy-done.3), kind=kLoop, calls=%fused_computation | loop fusion | flops 20971520 | bytes 41975872 | tf_op jit(solution)/shard_map/convert_element_type | solution.py:13
  54.0 0.0 copy-done
  54.0 0.0 all-gather.2.cloned.1.call-update
  54.0 0.0 copy-done.1
  54.0 0.0 copy-done.2
  54.0 7.3 %all_gather.10 = bf16[2048,8]{0,1:T(8,128)(2,1)S(1)} all-gather(bf16[512,8]{0,1:T(8,128)(2,1)S(1)} %multiply_convert_fusion), channel_id=1, replica_groups=mesh['expert'=8,'shard'=4] {'shard'}, dimensions={0}, use_global_device_ids=true | all-gather | bytes 40960 | tf_op jit(solution)/shard_map/all_gather | solution.py:16
  61.3 14.4 %all_gather.11 = bf16[2048,64]{0,1:T(8,128)(2,1)S(1)} all-gather(bf16[2048,8]{0,1:T(8,128)(2,1)S(1)} %all_gather.10), channel_id=1, replica_groups=mesh['expert'=8,'shard'=4] {'expert'}, dimensions={1}, use_global_device_ids=true | all-gather | bytes 294912 | tf_op jit(solution)/shard_map/all_gather | solution.py:17
  75.7 274.8 %all-gather.2.cloned.1.call-done = bf16[8,1024,2048]{2,1,0:T(8,128)(2,1)} async-done(((bf16[8,1024,512]{2,1,0:T(8,128)(2,1)}), bf16[8,1024,2048]{2,1,0:T(8,128)(2,1)}) %all-gather.2.cloned.1.call-update) | async-done | bytes 33554448 | tf_op jit(solution)/shard_map/all_gather | solution.py:14
  350.5 22.9 %copy.10 = bf16[8,1024,2048]{2,1,0:T(8,128)(2,1)} copy(bf16[8,1024,2048]{2,1,0:T(8,128)(2,1)} %all-gather.2.cloned.1.call-done) | data formatting | bytes 67108864
  373.4 0.7 copy.11
  (2 shorter events, 0.0 us)
Async XLA Ops:
  7.2 343.3 %all-gather.2.cloned.1.call-start = ((), (), s32[]{:S(2)}) async-start(), calls=%async_computation | async-start | bytes 41943040 | tf_op jit(solution)/shard_map/all_gather | solution.py:14
  7.9 31.0 %copy-start.3 = (f32[8]{0:T(128)S(1)}, f32[8]{0:T(128)}, u32[]{:S(2)}) copy-start(f32[8]{0:T(128)} %param.7) | copy-start | bytes 100
  38.9 15.1 %copy-start = (f32[8,1024]{1,0:T(8,128)}, f32[8,1024]{1,0:T(8,128)S(1)}, u32[]{:S(2)}) copy-start(f32[8,1024]{1,0:T(8,128)S(1)} %broadcast_multiply_fusion) | copy-start | bytes 98308
  38.9 15.1 %copy-start.1 = (f32[512,8]{0,1:T(8,128)S(1)}, f32[512,8]{0,1:T(8,128)}, u32[]{:S(2)}) copy-start(f32[512,8]{0,1:T(8,128)} %param.8) | copy-start | bytes 49156
  38.9 15.1 %copy-start.2 = (f32[512]{0:T(512)S(1)}, f32[512]{0:T(512)}, u32[]{:S(2)}) copy-start(f32[512]{0:T(512)} %param.9) | copy-start | bytes 6148
Sparse Core Ops, SparseCore 0:
  54.1 296.3 all-gather.1
where the time goes:
time: 381 us
  waiting for transfers between devices  275 us (72%)
  blocking collectives  39.5 us (10%)
  other arithmetic  28.9 us (8%)
  local copies, waits for them, and re-layouts  23.6 us (6%)
  between operations  14.1 us (4%)
    all_gather x1, waiting for transfers between devices, body(): serve_down = lax.all_gather(narrow_down, 'shard', axis=2, tiled=True)  275 us
    unnamed x10, local copies, waits for them, and re-layouts  23.6 us
    psum x1, blocking collectives, body(): total_down = lax.psum(jnp.sum(jnp.abs(fresh_down), axis=2), 'shard')  17.8 us
    convert_element_type x1, other arithmetic, body(): (fresh_down / jnp.expand_dims(scale_down, 2)).astype(jnp.bfloat16)  15.1 us
    all_gather x1, blocking collectives, body(): serve_router = lax.all_gather(row_router, 'expert', axis=1, tiled=True)  14.4 us
    reduce_sum x1, other arithmetic, body(): total_down = lax.psum(jnp.sum(jnp.abs(fresh_down), axis=2), 'shard')  13.2 us
  transfers between devices with their start and end apart: 1, of which 1 were waited for; matrix products, arithmetic and copies ran while one was open for 0% of the time, Pallas kernels for 0%

commit v1 on v0

v1 whole, which is shorter than its diff:
```python
import functools
import math

import jax
import jax.numpy as jnp
from jax import lax
from jax.experimental import pallas as pl
from jax.experimental.pallas import tpu as pltpu
from jax.sharding import PartitionSpec as P

MESH = pl.DeviceIdType.MESH
LANES = 128
LOADS = 3
LAG = 2


def gather_kernel(
    shards, groups, width,
    mix_ref, w_ref, avg_ref, rw_ref, rg_ref,
    out_ref, scale_ref, router_ref,
    w_buf, avg_buf, fresh, narrow, sums, scales, rbuf,
    load_sem, own_sem, sum_send, sum_recv,
    row_send, row_recv, col_send, col_recv,
    f0_send, f0_recv, f1_send, f1_recv,
    rl_sem, re_send, re_recv, rs_send, rs_recv, sc_sem,
):
    experts, rows, cols = w_ref.shape
    side = math.isqrt(shards)
    half = rows // 2
    blocks = rows // LANES
    tiles = cols // LANES
    me = lax.axis_index("shard")
    group = lax.axis_index("expert")
    r, c = me // side, me % side
    loads = min(LOADS, experts)

    def load(e):
        slot = lax.rem(e, loads)
        return (
            pltpu.make_async_copy(w_ref.at[e], w_buf.at[slot], load_sem.at[0, slot]),
            pltpu.make_async_copy(avg_ref.at[e], avg_buf.at[slot], load_sem.at[1, slot]),
        )

    for e in range(loads):
        for copy in load(e):
            copy.start()

    barrier = pltpu.get_barrier_semaphore()
    for k in range(1, shards):
        pl.semaphore_signal(barrier, inc=1, device_id={"shard": lax.rem(me + k, shards)}, device_id_type=MESH)
    for k in range(1, groups):
        pl.semaphore_signal(barrier, inc=1, device_id={"expert": lax.rem(group + k, groups)}, device_id_type=MESH)
    rbuf[...] = (rw_ref[...] * rg_ref[...]).astype(jnp.bfloat16)
    pl.semaphore_wait(barrier, shards + groups - 2)

    def remote(src, dst, send, recv, device):
        return pltpu.make_async_remote_copy(
            src_ref=src, dst_ref=dst, send_sem=send, recv_sem=recv, device_id=device, device_id_type=MESH
        )

    def sum_copy(k, e, owner):
        part = sums.at[owner, e]
        return remote(part, part, sum_send.at[k - 1, e], sum_recv.at[k - 1, e], {"shard": lax.rem(me + k, shards)})

    def place(e, h, owner):
        return out_ref.at[e, pl.ds(h * half, half), pl.ds(pl.multiple_of(owner * cols, LANES), cols)]

    def row_mate(j):
        return r * side + lax.rem(c + j, side)

    def col_mate(i):
        return lax.rem(r + i, side) * side + c

    def row_copy(j, e, h):
        return remote(
            narrow.at[e, pl.ds(h * half, half)], place(e, h, me),
            row_send.at[j - 1, 2 * e + h], row_recv.at[j - 1, 2 * e + h], {"shard": row_mate(j)},
        )

    def col_copy(i, e, h):
        return remote(
            narrow.at[e, pl.ds(h * half, half)], place(e, h, me),
            col_send.at[i - 1, 2 * e + h], col_recv.at[i - 1, 2 * e + h], {"shard": col_mate(i)},
        )

    def landed(e, h, owner, recv):
        spot = place(e, h, owner)
        remote(spot, spot, own_sem.at[0], recv, {"shard": row_mate(1)}).wait_recv()

    def f0_copy(j, i, e):
        spot = place(e, 0, row_mate(side - j))
        n = (j - 1) * (side - 1) + i - 1
        return remote(spot, spot, f0_send.at[n, e], f0_recv.at[n, e], {"shard": col_mate(i)})

    def f1_copy(j, i, e):
        spot = place(e, 1, col_mate(side - i))
        n = (j - 1) * (side - 1) + i - 1
        return remote(spot, spot, f1_send.at[n, e], f1_recv.at[n, e], {"shard": row_mate(j)})

    def far(j, i):
        return lax.rem(r + side - i, side) * side + lax.rem(c + side - j, side)

    def own_copy(e):
        return pltpu.make_async_copy(
            narrow.at[e], out_ref.at[e, :, pl.ds(pl.multiple_of(me * cols, LANES), cols)], own_sem.at[e]
        )

    def mix(e):
        slot, keep = lax.rem(e, loads), lax.rem(e, LAG + 1)
        for copy in load(e):
            copy.wait()
        share = mix_ref[e]
        rest = 1.0 - share

        @pl.loop(0, blocks)
        def _(b):
            at = pl.ds(pl.multiple_of(b * LANES, LANES), LANES)
            value = share * w_buf[slot, at, :] + rest * avg_buf[slot, at, :]
            fresh[keep, at, :] = value
            size = jnp.abs(value)
            part = size[:, :LANES]
            for t in range(1, tiles):
                part = part + size[:, t * LANES:(t + 1) * LANES]
            sums[me, e, pl.ds(b, 1), :] = jnp.sum(part.T, axis=0, keepdims=True)

        @pl.when(e + loads < experts)
        def _():
            for copy in load(e + loads):
                copy.start()

        for k in range(1, shards):
            sum_copy(k, e, me).start()

    def send(e):
        keep = lax.rem(e, LAG + 1)
        for k in range(1, shards):
            sum_copy(k, e, lax.rem(me + shards - k, shards)).wait_recv()

        @pl.loop(0, blocks)
        def _(b):
            at = pl.ds(pl.multiple_of(b * LANES, LANES), LANES)
            total = sums[0, e, pl.ds(b, 1), :]
            for s in range(1, shards):
                total = total + sums[s, e, pl.ds(b, 1), :]
            scale = total / width
            scales[e, pl.ds(b, 1), :] = scale
            inverse = jnp.broadcast_to(1.0 / scale, (LANES, LANES)).T
            for t in range(tiles):
                lane = slice(t * LANES, (t + 1) * LANES)
                narrow[e, at, lane] = (fresh[keep, at, lane] * inverse).astype(jnp.bfloat16)

        for step in range(2):
            for j in range(1, side):
                row_copy(j, e, step).start()
                col_copy(j, e, 1 - step).start()
        own_copy(e).start()

    router_own = pltpu.make_async_copy(rbuf, router_ref.at[me, group], rl_sem.at[0])

    def re_copy(k, owner):
        return remote(
            rbuf, router_ref.at[me, owner], re_send.at[k - 1], re_recv.at[k - 1],
            {"expert": lax.rem(group + k, groups)},
        )

    def rs_copy(k, owner):
        return remote(
            router_ref.at[owner], router_ref.at[owner], rs_send.at[k - 1], rs_recv.at[k - 1],
            {"shard": lax.rem(me + k, shards)},
        )

    @pl.loop(0, experts + LAG)
    def _(t):
        @pl.when(t < experts)
        def _():
            mix(t)

        @pl.when(t >= LAG)
        def _():
            send(t - LAG)

    scale_copy = pltpu.make_async_copy(scales, scale_ref, sc_sem.at[0])
    scale_copy.start()
    router_own.start()
    for k in range(1, groups):
        re_copy(k, group).start()
    router_own.wait()
    for k in range(1, groups):
        re_copy(k, lax.rem(group + groups - k, groups)).wait_recv()
    for k in range(1, shards):
        rs_copy(k, me).start()

    @pl.loop(0, experts)
    def _(e):
        for j in range(1, side):
            landed(e, 0, row_mate(side - j), row_recv.at[j - 1, 2 * e])
            for i in range(1, side):
                f0_copy(j, i, e).start()
        for i in range(1, side):
            landed(e, 1, col_mate(side - i), col_recv.at[i - 1, 2 * e + 1])
            for j in range(1, side):
                f1_copy(j, i, e).start()

    scale_copy.wait()
    for k in range(1, groups):
        re_copy(k, group).wait_send()
    for k in range(1, shards):
        rs_copy(k, me).wait_send()
        rs_copy(k, lax.rem(me + shards - k, shards)).wait_recv()

    @pl.loop(0, experts)
    def _(e):
        own_copy(e).wait()
        for k in range(1, shards):
            sum_copy(k, e, me).wait_send()
        for j in range(1, side):
            landed(e, 1, row_mate(side - j), row_recv.at[j - 1, 2 * e + 1])
            landed(e, 0, col_mate(side - j), col_recv.at[j - 1, 2 * e])
            for h in range(2):
                row_copy(j, e, h).wait_send()
                col_copy(j, e, h).wait_send()
        for j in range(1, side):
            for i in range(1, side):
                n = (j - 1) * (side - 1) + i - 1
                landed(e, 0, far(j, i), f0_recv.at[n, e])
                landed(e, 1, far(j, i), f1_recv.at[n, e])
                f0_copy(j, i, e).wait_send()
                f1_copy(j, i, e).wait_send()


def body(shards, groups, w_down, avg_down, mix_share, router_weight, router_gain):
    experts, rows, cols = w_down.shape
    side = math.isqrt(shards)
    width = shards * cols
    blocks = rows // LANES
    rw = router_weight.T
    rg = router_gain[None, :]
    dma = pltpu.SemaphoreType.DMA
    f32, bf16 = jnp.float32, jnp.bfloat16
    loads = min(LOADS, experts)
    hbm = pl.BlockSpec(memory_space=pl.ANY)
    vmem = pl.BlockSpec(memory_space=pltpu.VMEM)
    forwards = (side - 1) * (side - 1)
    serve, scale, router = pl.pallas_call(
        functools.partial(gather_kernel, shards, groups, float(width)),
        out_shape=(
            jax.ShapeDtypeStruct((experts, rows, width), bf16),
            jax.ShapeDtypeStruct((experts, blocks, LANES), f32),
            jax.ShapeDtypeStruct((shards, groups) + rw.shape, bf16),
        ),
        in_specs=[pl.BlockSpec(memory_space=pltpu.SMEM), hbm, hbm, vmem, vmem],
        out_specs=(hbm, hbm, hbm),
        scratch_shapes=[
            pltpu.VMEM((loads, rows, cols), f32),
            pltpu.VMEM((loads, rows, cols), f32),
            pltpu.VMEM((LAG + 1, rows, cols), f32),
            pltpu.VMEM((experts, rows, cols), bf16),
            pltpu.VMEM((shards, experts, blocks, LANES), f32),
            pltpu.VMEM((experts, blocks, LANES), f32),
            pltpu.VMEM(rw.shape, bf16),
            dma((2, loads)),
            dma((experts,)),
            dma((shards - 1, experts)),
            dma((shards - 1, experts)),
            dma((side - 1, 2 * experts)),
            dma((side - 1, 2 * experts)),
            dma((side - 1, 2 * experts)),
            dma((side - 1, 2 * experts)),
            dma((forwards, experts)),
            dma((forwards, experts)),
            dma((forwards, experts)),
            dma((forwards, experts)),
            dma((1,)),
            dma((groups - 1,)),
            dma((groups - 1,)),
            dma((shards - 1,)),
            dma((shards - 1,)),
            dma((1,)),
        ],
        compiler_params=pltpu.CompilerParams(collective_id=0, has_side_effects=True),
    )(mix_share, w_down, avg_down, rw, rg)
    router = router.transpose(0, 3, 1, 2).reshape(shards * rw.shape[1], groups * rw.shape[0])
    return serve, scale.reshape(experts, rows), router


def solution(mesh):
    return jax.shard_map(
        functools.partial(body, mesh.shape["shard"], mesh.shape["expert"]),
        mesh=mesh,
        in_specs=(
            P("expert", None, "shard"),
            P("expert", None, "shard"),
            P("expert"),
            P("shard", "expert"),
            P("shard"),
        ),
        out_specs=(P("expert", None, None), P("expert", None), P()),
        check_vma=False,
    )
```

time: 381 us -> 315 us (0.83)
  Pallas kernels: 0 us -> 288 us
  waiting for transfers between devices: 275 us -> 0 us
  blocking collectives: 39.5 us -> 0 us
  other arithmetic: 28.9 us -> 0 us
  between operations: 14.1 us -> 0.64 us
    pallas_call x0 -> x1, Pallas kernels: none -> 288 us  [body(): pl.pallas_call(functools.partial(gather_kernel, shards, groups, float(wid...]
    all_gather x1 -> x0, waiting for transfers between devices: 275 us -> none  [body(): serve_down = lax.all_gather(narrow_down, 'shard', axis=2, tiled=True)]
    all_gather x2 -> x0, blocking collectives: 21.7 us -> none  [the longest x1 14.4 us: body(): serve_router = lax.all_gather(row_router, 'expert', axis=1, tiled=True)]
    psum x1 -> x0, blocking collectives: 17.8 us -> none  [body(): total_down = lax.psum(jnp.sum(jnp.abs(fresh_down), axis=2), 'shard')]
    convert_element_type x2 -> x0, other arithmetic: 15.1 us -> none  [the longest x1 15.1 us: body(): (fresh_down / jnp.expand_dims(scale_down, 2)).astype(jnp.bfloat16)]
    reduce_sum x1 -> x0, other arithmetic: 13.2 us -> none  [body(): total_down = lax.psum(jnp.sum(jnp.abs(fresh_down), axis=2), 'shard')]
    unnamed x10 -> x3, local copies, waits for them, and re-layouts: 23.6 us -> 25 us
  transfers between devices with their start and end apart: 1 -> 0, of which waited for: 1 -> 0; matrix products, arithmetic and copies ran while one was open for 0% -> 0% of each run, Pallas kernels for 0% -> 0%
where the time goes in v1:
time: 315 us; the launch traced here: 314 us
  Pallas kernels  288 us (91%)
  local copies, waits for them, and re-layouts  26.2 us (8%)
    pallas_call x1, Pallas kernels, body(): pl.pallas_call(functools.partial(gather_kernel, shards, groups, float(wid...  288 us
    unnamed x3, local copies, waits for them, and re-layouts  25 us

profile of v1, /device:TPU:0, one launch (start us, length us, event | category | flops | bytes accessed | tf_op | source)
XLA Modules:
  0.0 314.4 jit_solution(14286489416478955705)
XLA Ops:
  0.6 287.6 %shard_map.76 = (bf16[8,1024,2048]{2,1,0:T(8,128)(2,1)}, f32[8,8,128]{2,1,0:T(8,128)}, bf16[4,8,8,512]{3,2,1,0:T(8,128)(2,1)}) custom-call(f32[8]{0:T(128)} %mix_ref.1, f32[8,1024,512]{2,1,0:T(8,128)} %w_ref.1, f32[8,1024,512]{2,1,0:T(8,128)} %avg_ref.1, f32[8,512]{1,0:T(8,128)} %bitcast.19, f32[1,512]{1,0:T(1,128)} %bitcast.20), custom_call_target="tpu_custom_call" | custom-call | tf_op jit(solution)/shard_map/pallas_call | solution.py:244
  288.3 1.4 copy.14
  289.6 1.2 copy.13
  290.8 0.8 copy.10
  291.6 22.9 %copy.16 = bf16[8,1024,2048]{2,1,0:T(8,128)(2,1)} copy(bf16[8,1024,2048]{2,1,0:T(8,128)(2,1)} %get-tuple-element.12) | data formatting | bytes 67108864
